TPU v7x, 32 devices: a whole 2x2x4 slice. The times are simulated.
32 devices in a mesh: gx: 4 (over z), gy: 8 (over y, x, core).
Axes of the slice: x: 2, y: 2, z: 4, core: 2. Of those that a mesh axis runs over, the one named last changes fastest.
Arguments:
- stored_vectors: bfloat16 [2, 16, 32, 4096], P(None, None, 'gx', 'gy'), may hold values from -4 to 4
- disorder: float32 [2, 32, 4096], P(None, 'gx', 'gy'), may hold values from -1.5 to 1.5
- vacancy: int32 [2, 32, 4096], P(None, 'gx', 'gy'), may hold values 0 or 1
- plan: int32 [32], replicated, may hold values from 0 to 31, as said below
Outputs:
- local_moments: float32 [4, 2, 32, 4096], P(None, None, 'gx', 'gy')
- trace_moments: float32 [4, 16], replicated
Inputs may be any that keep to these rules, and one draw needn't show every extreme that they name: plan is a permutation of 0 to 31; stored block b is held by the device at gy index b // 4. The 4 lattice blocks of one device come from 4 different devices, and the 4 stored blocks of one device go to 4 different devices.
All inputs are finite; a program needn't handle non-finite values. No bound on the sum of `vacancy` on one device may be relied on, other than what follows from the above.
Results may differ from a plain program's by a relative error of at most 0.0003.
Values may be sent and summed in bfloat16 or wider, within the bound.
A program may use at most 64 MiB of HBM per device.

v0:
```python
import jax
import jax.numpy as jnp
from jax import lax
from jax.sharding import PartitionSpec as P

BLOCK = 128
R = 16
TERMS = 4


HOP_NEAR = 1.0
HOP_NEXT = 0.3
TWIST_COS = 0.4535961214255773
TWIST_SIN = 0.8912073600614354
SPREAD = 6.5
NEAR_A = ((0, 0), (-1, 0), (0, -1))
NEAR_B = ((0, 0), (1, 0), (0, 1))
SECOND = ((1, 0), (-1, 1), (0, -1))


def extended(block, sides, width):
    for axis, dim in sides:
        count = lax.axis_size(axis)
        forward = [(i, i + 1) for i in range(count - 1)]
        forward.append((count - 1, 0))
        backward = [(target, source) for source, target in forward]
        low = lax.ppermute(
            lax.slice_in_dim(block, block.shape[dim] - width, None, axis=dim), axis, forward
        )
        high = lax.ppermute(lax.slice_in_dim(block, 0, width, axis=dim), axis, backward)
        block = jnp.concatenate([low, block, high], axis=dim)
    return block


def collect_sum(fetch, field, shifts):
    total = fetch(field, shifts[0])
    for shift in shifts[1:]:
        total = total + fetch(field, shift)
    return total


def hamilton(fetch, real, imag, onsite, keep):
    backs = tuple(((-a, -b) for a, b in SECOND))
    out_real = []
    out_imag = []
    for sublat, chiral, bonds in ((0, 1.0, NEAR_A), (1, -1.0, NEAR_B)):
        other = 1 - sublat
        near_real = collect_sum(fetch, real[other], bonds)
        forward_real = collect_sum(fetch, real[sublat], SECOND)
        backward_real = collect_sum(fetch, real[sublat], backs)
        centre_real = fetch(real[sublat], (0, 0))
        mixed_real = TWIST_COS * (forward_real + backward_real)
        mixed_imag = chiral * TWIST_SIN * (forward_real - backward_real)
        level = onsite[sublat][None]
        if imag is None:
            result_imag = HOP_NEXT * mixed_imag
        else:
            near_imag = collect_sum(fetch, imag[other], bonds)
            forward_imag = collect_sum(fetch, imag[sublat], SECOND)
            backward_imag = collect_sum(fetch, imag[sublat], backs)
            centre_imag = fetch(imag[sublat], (0, 0))
            mixed_real = mixed_real - chiral * TWIST_SIN * (forward_imag - backward_imag)
            mixed_imag = mixed_imag + TWIST_COS * (forward_imag + backward_imag)
            result_imag = level * centre_imag - HOP_NEAR * near_imag + HOP_NEXT * mixed_imag
        result_real = level * centre_real - HOP_NEAR * near_real + HOP_NEXT * mixed_real
        factor = keep[sublat][None] / SPREAD
        out_real.append(result_real * factor)
        out_imag.append(result_imag * factor)
    return (jnp.stack(out_real), jnp.stack(out_imag))


def local(stored_vectors, disorder, vacancy, plan):
    column = lax.axis_index("gy")
    columns = lax.axis_size("gy")
    vectors = stored_vectors.shape[1]
    width_x = stored_vectors.shape[2]
    width_y = stored_vectors.shape[3]
    blocks_here = width_y // BLOCK
    total_blocks = plan.shape[0]
    wanted = lax.dynamic_slice_in_dim(plan, column * blocks_here, blocks_here)
    pieces = stored_vectors.reshape(2, vectors, width_x, blocks_here, BLOCK)
    held = column * blocks_here + jnp.arange(blocks_here, dtype=jnp.int32)
    matches = (plan[None, :] == held[:, None]).astype(jnp.int32)
    target = jnp.sum(jnp.arange(total_blocks, dtype=jnp.int32)[None, :] * matches, axis=1)
    target_device = target // blocks_here
    sender = (jnp.arange(columns, dtype=jnp.int32)[:, None] == target_device[None, :]).astype(
        jnp.bfloat16
    )
    outgoing = jnp.einsum(
        "pb,srxbc->psrxc", sender, pieces, preferred_element_type=jnp.float32
    ).astype(jnp.bfloat16)
    incoming = lax.all_to_all(outgoing, "gy", split_axis=0, concat_axis=0, tiled=True)
    source_device = wanted // blocks_here
    picker = (jnp.arange(columns, dtype=jnp.int32)[None, :] == source_device[:, None]).astype(
        jnp.bfloat16
    )
    arranged = jnp.einsum("kp,psrxc->srxkc", picker, incoming, preferred_element_type=jnp.float32)
    lattice = arranged.reshape(2, vectors, width_x, width_y)
    keep = vacancy.astype(jnp.float32)
    start = lattice * keep[:, None]
    sites_total = 2 * width_x * lax.axis_size("gx") * width_y * columns

    def operate(real, imag):
        if imag is None:
            joined = real[None]
        else:
            joined = jnp.stack([real, imag])
        padded = extended(joined, (("gx", 3), ("gy", 4)), 1)

        def fetch(field, shift):
            return field[
                :, 1 + shift[0] : 1 + shift[0] + width_x, 1 + shift[1] : 1 + shift[1] + width_y
            ]

        padded_imag = None if imag is None else padded[1]
        return hamilton(fetch, padded[0], padded_imag, disorder, keep)

    locals_list = []
    partials = []

    def record(field_real):
        product = start * field_real
        locals_list.append(jnp.sum(product, axis=1) / R)
        partial_value = jnp.sum(product, axis=(0, 2, 3))
        partials.append(partial_value)

    previous_real, previous_imag = (start, None)
    current_real, current_imag = operate(start, None)
    record(current_real)
    for term in range(1, TERMS):
        image_real, image_imag = operate(current_real, current_imag)
        next_real = 2.0 * image_real - previous_real
        if previous_imag is None:
            next_imag = 2.0 * image_imag
        else:
            next_imag = 2.0 * image_imag - previous_imag
        previous_real, previous_imag = (current_real, current_imag)
        current_real, current_imag = (next_real, next_imag)
        record(current_real)
    summed = lax.psum(jnp.stack(partials), ("gx", "gy"))
    return (jnp.stack(locals_list), summed / sites_total)


def solution(mesh):
    placed = (P(None, None, "gx", "gy"), P(None, "gx", "gy"), P(None, "gx", "gy"), P())
    return jax.shard_map(
        local,
        mesh=mesh,
        in_specs=placed,
        out_specs=(P(None, None, "gx", "gy"), P()),
        check_vma=False,
    )
```

profile of v0, /device:TPU:0, one launch (start us, length us, event | category | flops | bytes accessed | tf_op | source)
XLA Modules:
  0.0 175.9 jit_solution(6712092812964053303)
XLA Ops:
  0.7 0.9 select_reduce_fusion
  1.6 0.4 convolution_convert_fusion
  2.0 0.9 copy.10
  2.9 5.2 %all-to-all-start = ((bf16[8,2,16,8,128]{4,3,2,1,0:T(8,128)(2,1)}), bf16[8,2,16,8,128]{4,3,2,1,0:T(8,128)(2,1)S(1)}, u32[]{:S(2)}, u32[]{:S(2)}) async-start(bf16[8,2,16,8,128]{4,3,2,1,0:T(8,128)(2,1)} %copy.10), calls=%async_computation | async-start | bytes 1048576 | tf_op jit(solution)/shard_map/all_to_all | solution.py:92
  8.2 0.6 convert_bitcast_fusion
  8.8 9.0 %all-to-all-done = bf16[8,2,16,8,128]{4,3,2,1,0:T(8,128)(2,1)S(1)} async-done(((bf16[8,2,16,8,128]{4,3,2,1,0:T(8,128)(2,1)}), bf16[8,2,16,8,128]{4,3,2,1,0:T(8,128)(2,1)S(1)}, u32[]{:S(2)}, u32[]{:S(2)}) %all-to-all-start) | async-done | bytes 524320 | tf_op jit(solution)/shard_map/all_to_all | solution.py:92
  17.8 0.4 convolution_bitcast_fusion
  18.6 1.6 collective-permute-start
  20.3 2.2 %collective-permute-start.1 = (f32[1,2,16,1,512]{4,3,2,1,0:T(1,128)S(1)}, f32[1,2,16,1,512]{4,3,2,1,0:T(1,128)S(1)}, u32[]{:S(2)}, u32[]{:S(2)}) collective-permute-start(f32[1,2,16,1,512]{4,3,2,1,0:T(1,128)S(1)} %get-tuple-element.54), channel_id=1, source_target_pairs={{8,0},{16,8},{24,16},{0,24},{9,1},{17,9},{25,17},{1,25},{10,2},{18... | collective-permute-start | bytes 196616 | tf_op jit(solution)/shard_map/ppermute | solution.py:30
  22.5 2.3 %collective-permute-done = f32[1,2,16,1,512]{4,3,2,1,0:T(1,128)S(1)} collective-permute-done((f32[1,2,16,1,512]{4,3,2,1,0:T(1,128)S(1)}, f32[1,2,16,1,512]{4,3,2,1,0:T(1,128)S(1)}, u32[]{:S(2)}, u32[]{:S(2)}) %collective-permute-start) | collective-permute-done | bytes 65568 | tf_op jit(solution)/shard_map/ppermute | solution.py:27
  24.9 0.4 collective-permute-done.1
  25.5 2.6 %collective-permute-start.3 = (f32[1,2,16,10,1]{4,3,2,1,0:T(8,128)S(1)}, f32[1,2,16,10,1]{4,3,2,1,0:T(8,128)S(1)}, u32[]{:S(2)}, u32[]{:S(2)}) collective-permute-start(f32[1,2,16,10,1]{4,3,2,1,0:T(8,128)S(1)} %get-tuple-element.48), channel_id=1, source_target_pairs={{1,0},{2,1},{3,2},{4,3},{5,4},{6,5},{7,6},{0,7},{9,8},{10,9},{11,1... | collective-permute-start | bytes 3848 | tf_op jit(solution)/shard_map/ppermute | solution.py:30
  28.1 6.8 %collective-permute-done.2 = f32[1,2,16,10,1]{4,3,2,1,0:T(8,128)S(1)} collective-permute-done((f32[1,2,16,10,1]{4,3,2,1,0:T(8,128)S(1)}, f32[1,2,16,10,1]{4,3,2,1,0:T(8,128)S(1)}, u32[]{:S(2)}, u32[]{:S(2)}) %collective-permute-start.2) | collective-permute-done | bytes 1312 | tf_op jit(solution)/shard_map/ppermute | solution.py:27
  35.0 0.9 pad_maximum_fusion.3
  36.0 0.6 fusion.40
  36.6 0.4 add_multiply_fusion.5
  37.3 0.7 collective-permute-start.4
  38.0 3.2 %collective-permute-start.5 = (f32[2,2,16,1,512]{4,3,2,1,0:T(1,128)S(1)}, f32[2,2,16,1,512]{4,3,2,1,0:T(1,128)S(1)}, u32[]{:S(2)}, u32[]{:S(2)}) collective-permute-start(f32[2,2,16,1,512]{4,3,2,1,0:T(1,128)S(1)} %get-tuple-element.46), channel_id=1, source_target_pairs={{8,0},{16,8},{24,16},{0,24},{9,1},{17,9},{25,17},{1,25},{10,2},{18... | collective-permute-start | bytes 393224 | tf_op jit(solution)/shard_map/ppermute | solution.py:30
  41.2 4.0 %collective-permute-done.4 = f32[2,2,16,1,512]{4,3,2,1,0:T(1,128)S(1)} collective-permute-done((f32[2,2,16,1,512]{4,3,2,1,0:T(1,128)S(1)}, f32[2,2,16,1,512]{4,3,2,1,0:T(1,128)S(1)}, u32[]{:S(2)}, u32[]{:S(2)}) %collective-permute-start.4) | collective-permute-done | bytes 131104 | tf_op jit(solution)/shard_map/ppermute | solution.py:27
  45.4 0.4 pad_maximum_fusion.15
  45.8 2.6 %collective-permute-start.7 = (f32[2,2,16,10,1]{4,3,2,1,0:T(8,128)S(1)}, f32[2,2,16,10,1]{4,3,2,1,0:T(8,128)S(1)}, u32[]{:S(2)}, u32[]{:S(2)}) collective-permute-start(f32[2,2,16,10,1]{4,3,2,1,0:T(8,128)S(1)} %get-tuple-element.33), channel_id=1, source_target_pairs={{1,0},{2,1},{3,2},{4,3},{5,4},{6,5},{7,6},{0,7},{9,8},{10,9},{11,1... | collective-permute-start | bytes 7688 | tf_op jit(solution)/shard_map/ppermute | solution.py:30
  48.5 11.6 %collective-permute-done.6 = f32[2,2,16,10,1]{4,3,2,1,0:T(8,128)S(1)} collective-permute-done((f32[2,2,16,10,1]{4,3,2,1,0:T(8,128)S(1)}, f32[2,2,16,10,1]{4,3,2,1,0:T(8,128)S(1)}, u32[]{:S(2)}, u32[]{:S(2)}) %collective-permute-start.6) | collective-permute-done | bytes 2592 | tf_op jit(solution)/shard_map/ppermute | solution.py:27
  60.0 1.9 %pad_maximum_fusion = f32[2,2,16,10,514]{4,3,2,1,0:T(8,128)S(1)} fusion(f32[2,2,16,10,1]{4,3,2,1,0:T(8,128)S(1)} %collective-permute-done.7, f32[2,2,16,1,512]{4,3,2,1,0:T(1,128)S(1)} %collective-permute-done.5, f32[1,2,16,8,512]{4,3,2,1,0:T(8,128)S(1)} %maximum_bitcast_fusion.1, f32[1,2,16,8,512]{4,3,2,1,0:T(8,128)S(1)} %maximum_bitcast_fusion, ...), kind=kLoop, calls=%fused_computation | loop fusion | flops 1644800 | bytes 2631680 | tf_op jit(solution)/shard_map/concatenate | solution.py:31
  62.1 0.8 add_multiply_fusion.3
  63.0 0.9 add_multiply_fusion.2
  63.8 0.8 multiply_bitcast_fusion.3
  64.7 0.9 multiply_bitcast_fusion.2
  65.9 2.1 %collective-permute-start.8 = (f32[2,2,16,1,512]{4,3,2,1,0:T(1,128)S(1)}, f32[2,2,16,1,512]{4,3,2,1,0:T(1,128)S(1)}, u32[]{:S(2)}, u32[]{:S(2)}) collective-permute-start(f32[2,2,16,1,512]{4,3,2,1,0:T(1,128)S(1)} %get-tuple-element.43), channel_id=1, source_target_pairs={{0,8},{8,16},{16,24},{24,0},{1,9},{9,17},{17,25},{25,1},{2,10},{10... | collective-permute-start | bytes 393224 | tf_op jit(solution)/shard_map/ppermute | solution.py:27
  68.0 1.8 %collective-permute-start.9 = (f32[2,2,16,1,512]{4,3,2,1,0:T(1,128)S(1)}, f32[2,2,16,1,512]{4,3,2,1,0:T(1,128)S(1)}, u32[]{:S(2)}, u32[]{:S(2)}) collective-permute-start(f32[2,2,16,1,512]{4,3,2,1,0:T(1,128)S(1)} %get-tuple-element.44), channel_id=1, source_target_pairs={{8,0},{16,8},{24,16},{0,24},{9,1},{17,9},{25,17},{1,25},{10,2},{18... | collective-permute-start | bytes 393224 | tf_op jit(solution)/shard_map/ppermute | solution.py:30
  69.8 4.4 %collective-permute-done.8 = f32[2,2,16,1,512]{4,3,2,1,0:T(1,128)S(1)} collective-permute-done((f32[2,2,16,1,512]{4,3,2,1,0:T(1,128)S(1)}, f32[2,2,16,1,512]{4,3,2,1,0:T(1,128)S(1)}, u32[]{:S(2)}, u32[]{:S(2)}) %collective-permute-start.8) | collective-permute-done | bytes 131104 | tf_op jit(solution)/shard_map/ppermute | solution.py:27
  74.2 1.9 %collective-permute-done.9 = f32[2,2,16,1,512]{4,3,2,1,0:T(1,128)S(1)} collective-permute-done((f32[2,2,16,1,512]{4,3,2,1,0:T(1,128)S(1)}, f32[2,2,16,1,512]{4,3,2,1,0:T(1,128)S(1)}, u32[]{:S(2)}, u32[]{:S(2)}) %collective-permute-start.9) | collective-permute-done | bytes 131104 | tf_op jit(solution)/shard_map/ppermute | solution.py:30
  76.1 0.4 pad_maximum_fusion.11
  76.5 2.6 %collective-permute-start.11 = (f32[2,2,16,10,1]{4,3,2,1,0:T(8,128)S(1)}, f32[2,2,16,10,1]{4,3,2,1,0:T(8,128)S(1)}, u32[]{:S(2)}, u32[]{:S(2)}) collective-permute-start(f32[2,2,16,10,1]{4,3,2,1,0:T(8,128)S(1)} %get-tuple-element.31), channel_id=1, source_target_pairs={{1,0},{2,1},{3,2},{4,3},{5,4},{6,5},{7,6},{0,7},{9,8},{10,9},{11,1... | collective-permute-start | bytes 7688 | tf_op jit(solution)/shard_map/ppermute | solution.py:30
  79.2 12.5 %collective-permute-done.10 = f32[2,2,16,10,1]{4,3,2,1,0:T(8,128)S(1)} collective-permute-done((f32[2,2,16,10,1]{4,3,2,1,0:T(8,128)S(1)}, f32[2,2,16,10,1]{4,3,2,1,0:T(8,128)S(1)}, u32[]{:S(2)}, u32[]{:S(2)}) %collective-permute-start.10) | collective-permute-done | bytes 2592 | tf_op jit(solution)/shard_map/ppermute | solution.py:27
  91.6 1.9 %pad_maximum_fusion.1 = f32[2,2,16,10,514]{4,3,2,1,0:T(8,128)S(1)} fusion(f32[2,2,16,10,1]{4,3,2,1,0:T(8,128)S(1)} %collective-permute-done.11, f32[2,2,16,1,512]{4,3,2,1,0:T(1,128)S(1)} %collective-permute-done.9, f32[1,2,16,8,512]{4,3,2,1,0:T(8,128)S(1)} %maximum_multiply_fusion.2, f32[1,2,16,8,512]{4,3,2,1,0:T(8,128)S(1)} %fusion.1, ...), kind=kLoop, calls=%fused_computation.1 | loop fusion | flops 1644800 | bytes 2631680 | tf_op jit(solution)/shard_map/concatenate | solution.py:31
  93.7 0.8 add_multiply_fusion.1
  94.6 0.9 add_multiply_fusion
  95.5 0.8 multiply_bitcast_fusion.1
  96.3 0.9 multiply_bitcast_fusion
  97.4 0.9 pad_maximum_fusion.20
  98.3 0.6 collective-permute-start.12
  98.9 3.2 %collective-permute-start.13 = (f32[2,2,16,1,512]{4,3,2,1,0:T(1,128)}, f32[2,2,16,1,512]{4,3,2,1,0:T(1,128)}, u32[]{:S(2)}, u32[]{:S(2)}) collective-permute-start(f32[2,2,16,1,512]{4,3,2,1,0:T(1,128)} %get-tuple-element.42), channel_id=1, source_target_pairs={{8,0},{16,8},{24,16},{0,24},{9,1},{17,9},{25,17},{1,25},{10,2},{18... | collective-permute-start | bytes 393224 | tf_op jit(solution)/shard_map/ppermute | solution.py:30
  102.1 0.6 copy.12
  102.7 0.8 stack.134
  103.5 0.8 stack.135
  104.2 1.0 constant_dynamic-update-slice_fusion.1
  105.3 1.5 collective-permute-done.12
  106.7 0.3 collective-permute-done.13
  107.0 2.1 %pad_maximum_fusion.7 = (f32[2,2,16,10,1]{4,3,2,1,0:T(8,128)}, f32[2,2,16,10,1]{4,3,2,1,0:T(8,128)}) fusion(f32[2,2,16,1,512]{4,3,2,1,0:T(1,128)} %collective-permute-done.13, f32[2,2,16,1,512]{4,3,2,1,0:T(1,128)} %collective-permute-done.12, f32[1,2,16,8,512]{4,3,2,1,0:T(8,128)S(1)} %fusion.5, f32[1,2,16,8,512]{4,3,2,1,0:T(8,128)S(1)} %fusion.4), kind=kLoop, calls=%fused_computation.23 | loop fusion | flops 3840 | bytes 1315840 | tf_op jit(solution)/shard_map/slice | solution.py:28
  109.1 2.6 %collective-permute-start.15 = (f32[2,2,16,10,1]{4,3,2,1,0:T(8,128)}, f32[2,2,16,10,1]{4,3,2,1,0:T(8,128)}, u32[]{:S(2)}, u32[]{:S(2)}) collective-permute-start(f32[2,2,16,10,1]{4,3,2,1,0:T(8,128)} %get-tuple-element.29), channel_id=1, source_target_pairs={{1,0},{2,1},{3,2},{4,3},{5,4},{6,5},{7,6},{0,7},{9,8},{10,9},{11,1... | collective-permute-start | bytes 7688 | tf_op jit(solution)/shard_map/ppermute | solution.py:30
  111.8 0.9 stack.146
  112.7 0.8 stack.147
  113.5 0.8 stack.156
  114.3 0.8 stack.157
  115.1 9.4 %collective-permute-done.14 = f32[2,2,16,10,1]{4,3,2,1,0:T(8,128)} collective-permute-done((f32[2,2,16,10,1]{4,3,2,1,0:T(8,128)}, f32[2,2,16,10,1]{4,3,2,1,0:T(8,128)}, u32[]{:S(2)}, u32[]{:S(2)}) %collective-permute-start.14) | collective-permute-done | bytes 2592 | tf_op jit(solution)/shard_map/ppermute | solution.py:27
  124.5 3.1 %pad_maximum_fusion.2 = f32[2,2,16,10,514]{4,3,2,1,0:T(8,128)S(1)} fusion(f32[2,2,16,10,1]{4,3,2,1,0:T(8,128)} %collective-permute-done.15, f32[2,2,16,1,512]{4,3,2,1,0:T(1,128)} %collective-permute-done.13, f32[1,2,16,8,512]{4,3,2,1,0:T(8,128)S(1)} %fusion.5, f32[1,2,16,8,512]{4,3,2,1,0:T(8,128)S(1)} %fusion.4, ...), kind=kLoop, calls=%fused_computation.2 | loop fusion | flops 1644800 | bytes 2631680 | tf_op jit(solution)/shard_map/concatenate | solution.py:31
  127.9 0.8 fusion.23
  128.7 0.8 stack.172
  129.5 2.4 %fusion.14 = f32[16,8,512]{2,1,0:T(8,128)} fusion(f32[16,10,514]{2,1,0:T(8,128)S(1)} %get-tuple-element.17, f32[16,10,514]{2,1,0:T(8,128)S(1)} %get-tuple-element.18, f32[16,10,514]{2,1,0:T(8,128)S(1)} %get-tuple-element.19, f32[8,512]{1,0:T(8,128)S(1)} %get-tuple-element.60, f32[8,512]{1,0:T(8,128)} %copy-done.5), kind=kLoop, calls=%fused_computation.58 | loop fusion | flops 1310720 | bytes 4489216 | tf_op jit(solution)/shard_map/mul | solution.py:67
  131.9 1.0 stack.173
  132.9 2.0 %fusion.38 = (f32[16]{0:T(128)S(1)}, f32[2,8,4,128]{3,2,1,0:T(4,128)S(1)}, f32[2,16,8,4,128]{4,3,2,1,0:T(4,128)S(1)}, f32[2,16,8,4,128]{4,3,2,1,0:T(4,128)S(1)}, f32[2,16,8,4,128]{4,3,2,1,0:T(4,128)S(1)}) fusion(f32[2,16,8,4,128]{4,3,2,1,0:T(4,128)S(1)} %copy-done.2, f32[2,16,8,4,128]{4,3,2,1,0:T(4,128)S(1)} %convolution_bitcast_fusion, ...), kind=kLoop, calls=%fused_computation.148 | loop fusion | flops 2088944 | bytes 4259904 | tf_op jit(solution)/shard_map/reduce_sum | solution.py:124
  135.7 38.9 %psum.7 = f32[4,16]{1,0:T(4,128)S(1)} all-reduce(f32[4,16]{1,0:T(4,128)S(1)} %pad_maximum_fusion.26), channel_id=1, replica_groups=mesh['gx'=4,'gy'=8] {'gx','gy'}, use_global_device_ids=true, to_apply=%region_9.10 | all-reduce | flops 64 | bytes 512 | tf_op jit(solution)/shard_map/psum | solution.py:140
  174.5 0.6 broadcast_multiply_fusion.7
  175.2 0.7 pad_maximum_fusion.25
  (63 shorter events, 3.4 us)
Async XLA Ops:
  0.6 1.0 copy-start
  0.6 7.5 %copy-start.9 = (s32[32]{0:T(128)S(1)}, s32[32]{0:T(128)}, u32[]{:S(2)}) copy-start(s32[32]{0:T(128)} %param.7) | copy-start | bytes 388
  0.7 7.6 %copy-start.7 = (s32[2,8,512]{2,1,0:T(8,128)S(1)}, s32[2,8,512]{2,1,0:T(8,128)}, u32[]{:S(2)}) copy-start(s32[2,8,512]{2,1,0:T(8,128)} %param.6) | copy-start | bytes 98308
  2.0 20.5 %copy-start.8 = (f32[2,8,512]{2,1,0:T(8,128)S(1)}, f32[2,8,512]{2,1,0:T(8,128)}, u32[]{:S(2)}) copy-start(f32[2,8,512]{2,1,0:T(8,128)} %param.5) | copy-start | bytes 98308
  2.9 14.9 %all-to-all-start = ((bf16[8,2,16,8,128]{4,3,2,1,0:T(8,128)(2,1)}), bf16[8,2,16,8,128]{4,3,2,1,0:T(8,128)(2,1)S(1)}, u32[]{:S(2)}, u32[]{:S(2)}) async-start(bf16[8,2,16,8,128]{4,3,2,1,0:T(8,128)(2,1)} %copy.10), calls=%async_computation | async-start | bytes 1048576 | tf_op jit(solution)/shard_map/all_to_all | solution.py:92
  18.6 6.2 %collective-permute-start = (f32[1,2,16,1,512]{4,3,2,1,0:T(1,128)S(1)}, f32[1,2,16,1,512]{4,3,2,1,0:T(1,128)S(1)}, u32[]{:S(2)}, u32[]{:S(2)}) collective-permute-start(f32[1,2,16,1,512]{4,3,2,1,0:T(1,128)S(1)} %get-tuple-element.53), channel_id=1, source_target_pairs={{0,8},{8,16},{16,24},{24,0},{1,9},{9,17},{17,25},{25,1},{2,10},{10... | collective-permute-start | bytes 196616 | tf_op jit(solution)/shard_map/ppermute | solution.py:27
  20.3 5.0 %collective-permute-start.1 = (f32[1,2,16,1,512]{4,3,2,1,0:T(1,128)S(1)}, f32[1,2,16,1,512]{4,3,2,1,0:T(1,128)S(1)}, u32[]{:S(2)}, u32[]{:S(2)}) collective-permute-start(f32[1,2,16,1,512]{4,3,2,1,0:T(1,128)S(1)} %get-tuple-element.54), channel_id=1, source_target_pairs={{8,0},{16,8},{24,16},{0,24},{9,1},{17,9},{25,17},{1,25},{10,2},{18... | collective-permute-start | bytes 196616 | tf_op jit(solution)/shard_map/ppermute | solution.py:30
  22.5 73.8 %copy-start.5 = (f32[8,512]{1,0:T(8,128)}, f32[8,512]{1,0:T(8,128)S(1)}, u32[]{:S(2)}) copy-start(f32[8,512]{1,0:T(8,128)S(1)} %get-tuple-element.66) | copy-start | bytes 49156
  25.4 9.6 %collective-permute-start.2 = (f32[1,2,16,10,1]{4,3,2,1,0:T(8,128)S(1)}, f32[1,2,16,10,1]{4,3,2,1,0:T(8,128)S(1)}, u32[]{:S(2)}, u32[]{:S(2)}) collective-permute-start(f32[1,2,16,10,1]{4,3,2,1,0:T(8,128)S(1)} %get-tuple-element.47), channel_id=1, source_target_pairs={{0,1},{1,2},{2,3},{3,4},{4,5},{5,6},{6,7},{7,0},{8,9},{9,10},{10,1... | collective-permute-start | bytes 3848 | tf_op jit(solution)/shard_map/ppermute | solution.py:27
  25.5 9.5 %collective-permute-start.3 = (f32[1,2,16,10,1]{4,3,2,1,0:T(8,128)S(1)}, f32[1,2,16,10,1]{4,3,2,1,0:T(8,128)S(1)}, u32[]{:S(2)}, u32[]{:S(2)}) collective-permute-start(f32[1,2,16,10,1]{4,3,2,1,0:T(8,128)S(1)} %get-tuple-element.48), channel_id=1, source_target_pairs={{1,0},{2,1},{3,2},{4,3},{5,4},{6,5},{7,6},{0,7},{9,8},{10,9},{11,1... | collective-permute-start | bytes 3848 | tf_op jit(solution)/shard_map/ppermute | solution.py:30
  37.3 7.9 %collective-permute-start.4 = (f32[2,2,16,1,512]{4,3,2,1,0:T(1,128)S(1)}, f32[2,2,16,1,512]{4,3,2,1,0:T(1,128)S(1)}, u32[]{:S(2)}, u32[]{:S(2)}) collective-permute-start(f32[2,2,16,1,512]{4,3,2,1,0:T(1,128)S(1)} %get-tuple-element.45), channel_id=1, source_target_pairs={{0,8},{8,16},{16,24},{24,0},{1,9},{9,17},{17,25},{25,1},{2,10},{10... | collective-permute-start | bytes 393224 | tf_op jit(solution)/shard_map/ppermute | solution.py:27
  38.0 7.4 %collective-permute-start.5 = (f32[2,2,16,1,512]{4,3,2,1,0:T(1,128)S(1)}, f32[2,2,16,1,512]{4,3,2,1,0:T(1,128)S(1)}, u32[]{:S(2)}, u32[]{:S(2)}) collective-permute-start(f32[2,2,16,1,512]{4,3,2,1,0:T(1,128)S(1)} %get-tuple-element.46), channel_id=1, source_target_pairs={{8,0},{16,8},{24,16},{0,24},{9,1},{17,9},{25,17},{1,25},{10,2},{18... | collective-permute-start | bytes 393224 | tf_op jit(solution)/shard_map/ppermute | solution.py:30
  45.8 14.2 %collective-permute-start.6 = (f32[2,2,16,10,1]{4,3,2,1,0:T(8,128)S(1)}, f32[2,2,16,10,1]{4,3,2,1,0:T(8,128)S(1)}, u32[]{:S(2)}, u32[]{:S(2)}) collective-permute-start(f32[2,2,16,10,1]{4,3,2,1,0:T(8,128)S(1)} %get-tuple-element.32), channel_id=1, source_target_pairs={{0,1},{1,2},{2,3},{3,4},{4,5},{5,6},{6,7},{7,0},{8,9},{9,10},{10,1... | collective-permute-start | bytes 7688 | tf_op jit(solution)/shard_map/ppermute | solution.py:27
  45.8 14.2 %collective-permute-start.7 = (f32[2,2,16,10,1]{4,3,2,1,0:T(8,128)S(1)}, f32[2,2,16,10,1]{4,3,2,1,0:T(8,128)S(1)}, u32[]{:S(2)}, u32[]{:S(2)}) collective-permute-start(f32[2,2,16,10,1]{4,3,2,1,0:T(8,128)S(1)} %get-tuple-element.33), channel_id=1, source_target_pairs={{1,0},{2,1},{3,2},{4,3},{5,4},{6,5},{7,6},{0,7},{9,8},{10,9},{11,1... | collective-permute-start | bytes 7688 | tf_op jit(solution)/shard_map/ppermute | solution.py:30
  65.9 8.3 %collective-permute-start.8 = (f32[2,2,16,1,512]{4,3,2,1,0:T(1,128)S(1)}, f32[2,2,16,1,512]{4,3,2,1,0:T(1,128)S(1)}, u32[]{:S(2)}, u32[]{:S(2)}) collective-permute-start(f32[2,2,16,1,512]{4,3,2,1,0:T(1,128)S(1)} %get-tuple-element.43), channel_id=1, source_target_pairs={{0,8},{8,16},{16,24},{24,0},{1,9},{9,17},{17,25},{25,1},{2,10},{10... | collective-permute-start | bytes 393224 | tf_op jit(solution)/shard_map/ppermute | solution.py:27
  68.0 8.1 %collective-permute-start.9 = (f32[2,2,16,1,512]{4,3,2,1,0:T(1,128)S(1)}, f32[2,2,16,1,512]{4,3,2,1,0:T(1,128)S(1)}, u32[]{:S(2)}, u32[]{:S(2)}) collective-permute-start(f32[2,2,16,1,512]{4,3,2,1,0:T(1,128)S(1)} %get-tuple-element.44), channel_id=1, source_target_pairs={{8,0},{16,8},{24,16},{0,24},{9,1},{17,9},{25,17},{1,25},{10,2},{18... | collective-permute-start | bytes 393224 | tf_op jit(solution)/shard_map/ppermute | solution.py:30
  76.5 15.2 %collective-permute-start.10 = (f32[2,2,16,10,1]{4,3,2,1,0:T(8,128)S(1)}, f32[2,2,16,10,1]{4,3,2,1,0:T(8,128)S(1)}, u32[]{:S(2)}, u32[]{:S(2)}) collective-permute-start(f32[2,2,16,10,1]{4,3,2,1,0:T(8,128)S(1)} %get-tuple-element.30), channel_id=1, source_target_pairs={{0,1},{1,2},{2,3},{3,4},{4,5},{5,6},{6,7},{7,0},{8,9},{9,10},{10,1... | collective-permute-start | bytes 7688 | tf_op jit(solution)/shard_map/ppermute | solution.py:27
  76.5 15.1 %collective-permute-start.11 = (f32[2,2,16,10,1]{4,3,2,1,0:T(8,128)S(1)}, f32[2,2,16,10,1]{4,3,2,1,0:T(8,128)S(1)}, u32[]{:S(2)}, u32[]{:S(2)}) collective-permute-start(f32[2,2,16,10,1]{4,3,2,1,0:T(8,128)S(1)} %get-tuple-element.31), channel_id=1, source_target_pairs={{1,0},{2,1},{3,2},{4,3},{5,4},{6,5},{7,6},{0,7},{9,8},{10,9},{11,1... | collective-permute-start | bytes 7688 | tf_op jit(solution)/shard_map/ppermute | solution.py:30
  97.2 4.9 %copy-start.6 = (f32[2,8,4,128]{3,1,2,0:T(8,128)S(1)}, f32[2,8,4,128]{3,1,2,0:T(8,128)}, u32[]{:S(2)}) copy-start(f32[2,8,4,128]{3,1,2,0:T(8,128)} %get-tuple-element.55) | copy-start | bytes 98308
  98.3 8.5 %collective-permute-start.12 = (f32[2,2,16,1,512]{4,3,2,1,0:T(1,128)}, f32[2,2,16,1,512]{4,3,2,1,0:T(1,128)}, u32[]{:S(2)}, u32[]{:S(2)}) collective-permute-start(f32[2,2,16,1,512]{4,3,2,1,0:T(1,128)} %get-tuple-element.41), channel_id=1, source_target_pairs={{0,8},{8,16},{16,24},{24,0},{1,9},{9,17},{17,25},{25,1},{2,10},{10... | collective-permute-start | bytes 393224 | tf_op jit(solution)/shard_map/ppermute | solution.py:27
  98.9 8.1 %collective-permute-start.13 = (f32[2,2,16,1,512]{4,3,2,1,0:T(1,128)}, f32[2,2,16,1,512]{4,3,2,1,0:T(1,128)}, u32[]{:S(2)}, u32[]{:S(2)}) collective-permute-start(f32[2,2,16,1,512]{4,3,2,1,0:T(1,128)} %get-tuple-element.42), channel_id=1, source_target_pairs={{8,0},{16,8},{24,16},{0,24},{9,1},{17,9},{25,17},{1,25},{10,2},{18... | collective-permute-start | bytes 393224 | tf_op jit(solution)/shard_map/ppermute | solution.py:30
  104.2 7.5 %copy-start.4 = (f32[1,16,8,4,128]{4,3,2,1,0:T(4,128)S(1)}, f32[1,16,8,4,128]{4,3,2,1,0:T(4,128)}, u32[]{:S(2)}) copy-start(f32[1,16,8,4,128]{4,3,2,1,0:T(4,128)} %stack.135) | copy-start | bytes 786436
  109.1 15.4 %collective-permute-start.14 = (f32[2,2,16,10,1]{4,3,2,1,0:T(8,128)}, f32[2,2,16,10,1]{4,3,2,1,0:T(8,128)}, u32[]{:S(2)}, u32[]{:S(2)}) collective-permute-start(f32[2,2,16,10,1]{4,3,2,1,0:T(8,128)} %get-tuple-element.28), channel_id=1, source_target_pairs={{0,1},{1,2},{2,3},{3,4},{4,5},{5,6},{6,7},{7,0},{8,9},{9,10},{10,1... | collective-permute-start | bytes 7688 | tf_op jit(solution)/shard_map/ppermute | solution.py:27
  109.1 15.4 %collective-permute-start.15 = (f32[2,2,16,10,1]{4,3,2,1,0:T(8,128)}, f32[2,2,16,10,1]{4,3,2,1,0:T(8,128)}, u32[]{:S(2)}, u32[]{:S(2)}) collective-permute-start(f32[2,2,16,10,1]{4,3,2,1,0:T(8,128)} %get-tuple-element.29), channel_id=1, source_target_pairs={{1,0},{2,1},{3,2},{4,3},{5,4},{6,5},{7,6},{0,7},{9,8},{10,9},{11,1... | collective-permute-start | bytes 7688 | tf_op jit(solution)/shard_map/ppermute | solution.py:30
  111.8 12.7 %copy-start.1 = (f32[2,16,8,4,128]{4,3,2,1,0:T(4,128)}, f32[2,16,8,4,128]{4,3,2,1,0:T(4,128)S(1)}, u32[]{:S(2)}) copy-start(f32[2,16,8,4,128]{4,3,2,1,0:T(4,128)S(1)} %constant_dynamic-update-slice_fusion) | copy-start | bytes 1572868
  129.5 3.4 %copy-start.2 = (f32[2,16,8,4,128]{4,3,2,1,0:T(4,128)S(1)}, f32[2,16,8,4,128]{4,3,2,1,0:T(4,128)}, u32[]{:S(2)}) copy-start(f32[2,16,8,4,128]{4,3,2,1,0:T(4,128)} %copy-done.1) | copy-start | bytes 1572868
  129.5 3.4 %copy-start.3 = (f32[1,16,8,4,128]{4,3,2,1,0:T(4,128)S(1)}, f32[1,16,8,4,128]{4,3,2,1,0:T(4,128)}, u32[]{:S(2)}) copy-start(f32[1,16,8,4,128]{4,3,2,1,0:T(4,128)} %stack.146) | copy-start | bytes 786436
where the time goes:
time: 176 us
  waiting for transfers between devices  64.3 us (37%)
  blocking collectives  38.9 us (22%)
  starting transfers between devices  31.4 us (18%)
  other arithmetic  29.2 us (17%)
  local copies, waits for them, and re-layouts  10.3 us (6%)
    ppermute x8, waiting for transfers between devices, extended(): lax.ppermute(lax.slice_in_dim(block, block.shape[dim] - width, None, axis...  52.5 us
    psum x1, blocking collectives, local(): summed = lax.psum(jnp.stack(partials), ('gx', 'gy'))  38.9 us
    ppermute x8, starting transfers between devices, extended(): lax.ppermute(lax.slice_in_dim(block, 0, width, axis=dim), axis, backward)  21 us
    all_to_all x1, waiting for transfers between devices, local(): lax.all_to_all(outgoing, 'gy', split_axis=0, concat_axis=0, tiled=True)  8.99 us
    concatenate x4, other arithmetic, extended(): block = jnp.concatenate([low, block, high], axis=dim)  7.79 us
    mul x8, other arithmetic, hamilton(): out_real.append(result_real * factor)  7.05 us
    another operation x9, local copies, waits for them, and re-layouts, hamilton(): return (jnp.stack(out_real), jnp.stack(out_imag))  6.65 us
    all_to_all x1, starting transfers between devices, local(): lax.all_to_all(outgoing, 'gy', split_axis=0, concat_axis=0, tiled=True)  5.2 us
  transfers between devices with their start and end apart: 17, of which 13 were waited for; matrix products, arithmetic and copies ran while one was open for 4% of the time, Pallas kernels for 0%

commit v1 on v0

v1 whole, which is shorter than its diff:
```python
import functools

import jax
import jax.numpy as jnp
from jax import lax
from jax.experimental import pallas as pl
from jax.experimental.pallas import tpu as pltpu
from jax.sharding import PartitionSpec as P

BLOCK = 128
TERMS = 4
HOP_NEXT = 0.3
TWIST_COS = 0.4535961214255773
TWIST_SIN = 0.8912073600614354
SPREAD = 6.5
HALO = TERMS
MESH = pl.DeviceIdType.MESH
F32 = jnp.float32

WAYS = tuple((a, b) for a in (-1, 0, 1) for b in (-1, 0, 1) if (a, b) != (0, 0))


def rows_from(a, wide):
    if a == 0:
        return slice(HALO, HALO + wide)
    return slice(0, HALO) if a == 1 else slice(HALO + wide, 2 * HALO + wide)


def rows_to(a, wide):
    if a == 0:
        return slice(0, wide)
    return slice(wide - HALO, wide) if a == 1 else slice(0, HALO)


def exchange(
    nx, ny,
    plan_ref, stored_ref, disorder_ref, vacancy_ref,
    lattice_ref, level_ref, keep_ref,
    turned, send, recv, grid, side, level_x, level_y, vac_x, vac_y,
    a2a_send, a2a_recv, halo_send, halo_recv, site_send, site_recv,
):
    gx, gy = lax.axis_index("gx"), lax.axis_index("gy")
    wide, long = disorder_ref.shape[1], disorder_ref.shape[2]
    blocks = long // BLOCK

    def at(a, b):
        return (lax.rem(gx + a + nx, nx), lax.rem(gy + b + ny, ny))

    def copy(source, target, out_sem, in_sem, device):
        return pltpu.make_async_remote_copy(
            src_ref=source, dst_ref=target, send_sem=out_sem, recv_sem=in_sem,
            device_id=device, device_id_type=MESH,
        )

    barrier = pltpu.get_barrier_semaphore()
    greeted = [at(0, i) for i in range(1, ny)] + [at(a, b) for a, b in WAYS if a != 0]
    for device in greeted:
        pl.semaphore_signal(barrier, inc=1, device_id=device, device_id_type=MESH)

    for k in range(blocks):
        for s in range(2):
            piece = stored_ref[s, :, :, k * BLOCK : (k + 1) * BLOCK].astype(F32)
            turned[k, s] = jnp.transpose(piece, (1, 0, 2)).astype(jnp.bfloat16)

    def fill(target, place):
        block = turned[0]
        for k in range(1, blocks):
            wanted = plan_ref[target * blocks] == gy * blocks + k
            for j in range(1, blocks):
                wanted = wanted | (plan_ref[target * blocks + j] == gy * blocks + k)
            block = jnp.where(wanted, turned[k], block)
        place[...] = block

    order = list(range(1, ny))
    for i in order:
        fill(lax.rem(gy + i, ny), send.at[i])
    pl.semaphore_wait(barrier, len(greeted))
    moves = []
    for i in order:
        move = copy(send.at[i], recv.at[gy], a2a_send.at[i], a2a_recv.at[i], at(0, i))
        move.start()
        moves.append(move)
    sites = []
    for w, (a, b) in enumerate(WAYS):
        lanes = slice(0, long) if b == 0 else (
            slice(long - BLOCK, long) if b == 1 else slice(0, BLOCK))
        for t, (own, by_x, by_y) in enumerate(
            ((disorder_ref, level_x, level_y), (vacancy_ref, vac_x, vac_y))
        ):
            target = by_x.at[w] if b == 0 else by_y.at[w]
            move = copy(own.at[:, :, lanes], target, site_send.at[w, t], site_recv.at[w, t],
                        at(a, b))
            move.start()
            sites.append(move)
    fill(gy, recv.at[gy])

    for move in sites:
        move.wait()
    low = lax.broadcasted_iota(jnp.int32, (2, wide, BLOCK), 2) < BLOCK // 2
    for own, by_x, by_y, out in (
        (disorder_ref, level_x, level_y, level_ref),
        (vacancy_ref, vac_x, vac_y, keep_ref),
    ):
        for a in (-1, 0, 1):
            middle = own[...] if a == 0 else by_x[WAYS.index((a, 0))]
            edge = jnp.where(low, by_y[WAYS.index((a, -1))], by_y[WAYS.index((a, 1))])
            kept = rows_to(a, wide)
            out[:, rows_from(a, wide), 0:long] = middle[:, kept].astype(F32)
            out[:, rows_from(a, wide), long:] = edge[:, kept].astype(F32)

    for move in moves:
        move.wait()
    for k in range(blocks):
        stored = plan_ref[gy * blocks + k]
        block = recv[0]
        for p in range(1, ny):
            block = jnp.where(stored >= p * blocks, recv[p], block)
        grid[:, HALO : HALO + wide, :, k * BLOCK : (k + 1) * BLOCK] = block
    halos = []
    for w, (a, b) in enumerate(WAYS):
        own = rows_to(a, wide)
        rows = slice(own.start + HALO, own.stop + HALO)
        if b == 0:
            source, target = grid.at[:, rows, :, 0:long], grid.at[:, rows_from(a, wide), :, 0:long]
        else:
            lanes = slice(long - BLOCK, long) if b == 1 else slice(0, BLOCK)
            source = grid.at[:, rows, :, lanes]
            target = side.at[0 if b == -1 else 1, :, rows_from(a, wide)]
        move = copy(source, target, halo_send.at[w], halo_recv.at[w], at(a, b))
        move.start()
        halos.append(move)
    for move in halos:
        move.wait()
    low = lax.broadcasted_iota(jnp.int32, grid.shape[:3] + (BLOCK,), 3) < BLOCK // 2
    lattice_ref[:, :, :, 0:long] = grid[...]
    lattice_ref[:, :, :, long:] = jnp.where(
        low, side[0].astype(F32), side[1].astype(F32)).astype(jnp.bfloat16)


def chebyshev(
    lattice_ref, level_ref, keep_ref, moments_ref, trace_ref,
    real0, imag0, real1, imag1, onsite, factor, traces,
):
    tall, vectors, extent = lattice_ref.shape[1:]
    wide, long = moments_ref.shape[2], moments_ref.shape[3]
    halves = vectors // 8
    cos, sin = HOP_NEXT * TWIST_COS, HOP_NEXT * TWIST_SIN

    factor[...] = keep_ref[...] * (1.0 / SPREAD)
    onsite[...] = level_ref[...] * factor[...]
    traces[...] = jnp.zeros_like(traces)

    @pl.loop(0, tall)
    def _(x):
        for s in range(2):
            mask = keep_ref[s, pl.ds(x, 1), :]
            real0[s, x] = lattice_ref[s, x].astype(F32) * mask

    def back(value):
        return pltpu.roll(value, 1, axis=1)

    def ahead(value):
        return pltpu.roll(value, extent - 1, axis=1)

    def bond(r, i, first, second, chiral, want_imag):
        turn = chiral * sin
        out_real = cos * (r[first] + r[second])
        if i is not None:
            out_real = out_real - turn * (i[first] - i[second])
        out_imag = None
        if want_imag:
            out_imag = turn * (r[first] - r[second])
            if i is not None:
                out_imag = out_imag + cos * (i[first] + i[second])
        return out_real, out_imag

    for n in range(1, TERMS + 1):
        cur_r, cur_i = (real0, imag0) if n % 2 else (real1, imag1)
        new_r, new_i = (real1, imag1) if n % 2 else (real0, imag0)
        complex_in, want_imag, keep_new = n > 1, n < TERMS, n < TERMS

        def row(x, half, measured):
            r8 = pl.ds(half * 8, 8)
            reals = [[cur_r[s, x + d, r8, :] for d in (-1, 0, 1)] for s in range(2)]
            imags = [None, None]
            if complex_in:
                imags = [[cur_i[s, x + d, r8, :] for d in (-1, 0, 1)] for s in range(2)]
            for s, chiral in ((0, 1.0), (1, -1.0)):
                r, i = reals[s], imags[s]
                other_r, other_i = reals[1 - s], imags[1 - s]
                here = bond(r, i, 2, 0, chiral, want_imag)
                behind = bond(r, i, 1, 2, chiral, want_imag)
                front = bond(r, i, 0, 1, chiral, want_imag)
                level = onsite[s, pl.ds(x, 1), :]
                scale = factor[s, pl.ds(x, 1), :]
                if n > 1:
                    level, scale = 2.0 * level, 2.0 * scale
                away = 0 if s == 0 else 2
                for part in range(2 if want_imag else 1):
                    own, other = (r, other_r) if part == 0 else (i, other_i)
                    hop, prior, later = here[part], behind[part], front[part]
                    if other is not None:
                        hop = hop - (other[1] + other[away])
                        if s == 0:
                            prior = prior - other[1]
                        else:
                            later = later - other[1]
                    result = (hop + (back(prior) + ahead(later))) * scale
                    if own is not None:
                        result = result + level * own[1]
                    store = new_r if part == 0 else new_i
                    if n == 2 and part == 0 or n > 2:
                        result = result - store[s, x, r8, :]
                    if keep_new:
                        store[s, x, r8, :] = result
                    if part == 0 and measured is not None:
                        start = lattice_ref[s, x].astype(F32)[half * 8 : half * 8 + 8]
                        start = start * keep_ref[s, pl.ds(x, 1), :]
                        measured(s, half, start[:, :long] * result[:, :long])

        def plain(x, carry):
            for half in range(halves):
                row(x, half, None)
            return carry

        def middle(x, carry):
            sums = [None, None]

            def measured(s, half, product):
                sums[s] = product if sums[s] is None else sums[s] + product
                total = traces[n - 1, half * 8 : half * 8 + 8, :]
                for k in range(long // BLOCK):
                    total = total + product[:, k * BLOCK : (k + 1) * BLOCK]
                traces[n - 1, half * 8 : half * 8 + 8, :] = total

            for half in range(halves):
                row(x, half, measured)
            for s in range(2):
                moments_ref[n - 1, s, pl.ds(x - HALO, 1), :] = (
                    jnp.sum(sums[s], axis=0, keepdims=True) * (1.0 / vectors))
            return carry

        if n < TERMS:
            lax.fori_loop(n, HALO, plain, 0)
        lax.fori_loop(HALO, HALO + wide, middle, 0)
        if n < TERMS:
            lax.fori_loop(HALO + wide, tall - n, plain, 0)

    lane = lax.broadcasted_iota(jnp.int32, (vectors, BLOCK), 1)
    gathered = jnp.zeros((vectors, BLOCK), F32)
    for n in range(TERMS):
        gathered = jnp.where(lane == n, jnp.sum(traces[n], axis=1, keepdims=True), gathered)
    trace_ref[...] = gathered


def local(nx, ny, stored_vectors, disorder, vacancy, plan):
    vectors, wide, long = stored_vectors.shape[1:]
    tall, extent = wide + 2 * HALO, long + BLOCK
    vmem = pl.BlockSpec(memory_space=pltpu.VMEM)
    bf16, i32 = jnp.bfloat16, jnp.int32
    dma = pltpu.SemaphoreType.DMA
    ways = len(WAYS)
    lattice, level, keep = pl.pallas_call(
        functools.partial(exchange, nx, ny),
        out_shape=(
            jax.ShapeDtypeStruct((2, tall, vectors, extent), bf16),
            jax.ShapeDtypeStruct((2, tall, extent), F32),
            jax.ShapeDtypeStruct((2, tall, extent), F32),
        ),
        in_specs=[pl.BlockSpec(memory_space=pltpu.SMEM), vmem, vmem, vmem],
        out_specs=(vmem,) * 3,
        scratch_shapes=[
            pltpu.VMEM((long // BLOCK, 2, wide, vectors, BLOCK), bf16),
            pltpu.VMEM((ny, 2, wide, vectors, BLOCK), bf16),
            pltpu.VMEM((ny, 2, wide, vectors, BLOCK), bf16),
            pltpu.VMEM((2, tall, vectors, long), bf16),
            pltpu.VMEM((2, 2, tall, vectors, BLOCK), bf16),
            pltpu.VMEM((ways, 2, wide, long), F32),
            pltpu.VMEM((ways, 2, wide, BLOCK), F32),
            pltpu.VMEM((ways, 2, wide, long), i32),
            pltpu.VMEM((ways, 2, wide, BLOCK), i32),
            dma((ny,)), dma((ny,)), dma((ways,)), dma((ways,)), dma((ways, 2)), dma((ways, 2)),
        ],
        compiler_params=pltpu.CompilerParams(collective_id=0, has_side_effects=True),
        name="exchange",
    )(plan, stored_vectors, disorder, vacancy)
    moments, trace = pl.pallas_call(
        chebyshev,
        out_shape=(
            jax.ShapeDtypeStruct((TERMS, 2, wide, long), F32),
            jax.ShapeDtypeStruct((vectors, BLOCK), F32),
        ),
        in_specs=[vmem] * 3,
        out_specs=(vmem,) * 2,
        scratch_shapes=[pltpu.VMEM((2, tall, vectors, extent), F32)] * 4
        + [pltpu.VMEM((2, tall, extent), F32)] * 2
        + [pltpu.VMEM((TERMS, vectors, BLOCK), F32)],
        name="chebyshev",
    )(lattice, level, keep)
    summed = lax.psum(trace[:, :TERMS].T, ("gx", "gy"))
    return moments, summed / (2 * wide * nx * long * ny)


def solution(mesh):
    placed = (P(None, None, "gx", "gy"), P(None, "gx", "gy"), P(None, "gx", "gy"), P())
    return jax.shard_map(
        functools.partial(local, mesh.shape["gx"], mesh.shape["gy"]),
        mesh=mesh,
        in_specs=placed,
        out_specs=(P(None, None, "gx", "gy"), P()),
        check_vma=False,
    )
```

time: 176 us -> 78.3 us (0.44)
  waiting for transfers between devices: 64.3 us -> 0 us
  Pallas kernels: 0 us -> 38.4 us
  starting transfers between devices: 31.4 us -> 0 us
  other arithmetic: 29.2 us -> 0.01 us
  local copies, waits for them, and re-layouts: 10.3 us -> 1.35 us
    ppermute x16 -> x0, waiting for transfers between devices: 55.3 us -> none  [the longest x8 52.5 us: extended(): lax.ppermute(lax.slice_in_dim(block, block.shape[dim] - width, None, axis...]
    pallas_call x0 -> x2, Pallas kernels: none -> 38.4 us  [the longest x1 29 us: local(): pl.pallas_call(functools.partial(exchange, nx, ny), out_shape=(jax.ShapeD...]
    ppermute x16 -> x0, starting transfers between devices: 26.2 us -> none  [the longest x8 21 us: extended(): lax.ppermute(lax.slice_in_dim(block, 0, width, axis=dim), axis, backward)]
    all_to_all x1 -> x0, waiting for transfers between devices: 8.99 us -> none  [local(): lax.all_to_all(outgoing, 'gy', split_axis=0, concat_axis=0, tiled=True)]
    concatenate x4 -> x0, other arithmetic: 7.79 us -> none  [extended(): block = jnp.concatenate([low, block, high], axis=dim)]
    mul x12 -> x0, other arithmetic: 7.76 us -> none  [the longest x8 7.05 us: hamilton(): out_real.append(result_real * factor)]
    another operation x9 -> x0, local copies, waits for them, and re-layouts: 6.65 us -> none  [hamilton(): return (jnp.stack(out_real), jnp.stack(out_imag))]
    all_to_all x1 -> x0, starting transfers between devices: 5.2 us -> none  [local(): lax.all_to_all(outgoing, 'gy', split_axis=0, concat_axis=0, tiled=True)]
  transfers between devices with their start and end apart: 17 -> 0, of which waited for: 13 -> 0; matrix products, arithmetic and copies ran while one was open for 4% -> 0% of each run, Pallas kernels for 0% -> 0%
where the time goes in v1:
time: 78.3 us; the launch traced here: 78 us
  Pallas kernels  38.4 us (49%)
  blocking collectives  37.6 us (48%)
  local copies, waits for them, and re-layouts  1.35 us (2%)
    psum x1, blocking collectives, local(): summed = lax.psum(trace[:, :TERMS].T, ('gx', 'gy'))  37.6 us
    pallas_call x1, Pallas kernels, local(): pl.pallas_call(functools.partial(exchange, nx, ny), out_shape=(jax.ShapeD...  29 us
    pallas_call x1, Pallas kernels, local(): pl.pallas_call(chebyshev, out_shape=(jax.ShapeDtypeStruct((TERMS, 2, wide...  9.37 us

profile of v1, /device:TPU:0, one launch (start us, length us, event | category | flops | bytes accessed | tf_op | source)
XLA Modules:
  0.0 78.0 jit_solution(8762021014922841565)
XLA Ops:
  0.6 29.0 %exchange.1 = (bf16[2,16,16,640]{3,2,1,0:T(8,128)(2,1)}, f32[2,16,640]{2,1,0:T(8,128)}, f32[2,16,640]{2,1,0:T(8,128)}) custom-call(s32[32]{0:T(128)} %plan_ref.1, bf16[2,16,8,512]{3,2,1,0:T(8,128)(2,1)} %stored_ref.1, f32[2,8,512]{2,1,0:T(8,128)} %disorder_ref.1, s32[2,8,512]{2,1,0:T(8,128)} %vacancy_ref.1), custom_call_target="tpu_custom_call" | custom-call | tf_op jit(solution)/shard_map/exchange/pallas_call | solution.py:263
  29.6 9.4 %chebyshev.1 = (f32[4,2,8,512]{3,2,1,0:T(8,128)}, f32[16,128]{1,0:T(8,128)}) custom-call(bf16[2,16,16,640]{3,2,1,0:T(8,128)(2,1)} %get-tuple-element.7.lattice_ref, f32[2,16,640]{2,1,0:T(8,128)} %get-tuple-element.8.level_ref, f32[2,16,640]{2,1,0:T(8,128)} %get-tuple-element.9.keep_ref), custom_call_target="tpu_custom_call" | custom-call | tf_op jit(solution)/shard_map/chebyshev/pallas_call | solution.py:287
  39.0 0.7 slice_bitcast_fusion
  39.7 37.6 %psum.7 = f32[4,16]{0,1:T(8,128)S(1)} all-reduce(f32[4,16]{0,1:T(8,128)S(1)} %slice_bitcast_fusion), channel_id=1, replica_groups=mesh['gx'=4,'gy'=8] {'gx','gy'}, use_global_device_ids=true, to_apply=%region_0.0 | all-reduce | flops 64 | bytes 512 | tf_op jit(solution)/shard_map/psum | solution.py:300
  77.4 0.7 copy.6
  (1 shorter events, 0.0 us)

commit v2 on v1

--- a/solution.py
+++ b/solution.py
@@ -32,16 +32,20 @@
     return slice(wide - HALO, wide) if a == 1 else slice(0, HALO)
 
 
-def exchange(
+def program(
     nx, ny,
     plan_ref, stored_ref, disorder_ref, vacancy_ref,
-    lattice_ref, level_ref, keep_ref,
-    turned, send, recv, grid, side, level_x, level_y, vac_x, vac_y,
-    a2a_send, a2a_recv, halo_send, halo_recv, site_send, site_recv,
+    moments_ref, trace_ref,
+    turned, send, recv, lattice, side, level_x, level_y, vac_x, vac_y, keep_ref, onsite, factor,
+    real0, imag0, real1, imag1, traces, part, parts_y, parts_x,
+    a2a_send, a2a_recv, halo_send, halo_recv, site_send, site_recv, sum_send, sum_recv,
 ):
     gx, gy = lax.axis_index("gx"), lax.axis_index("gy")
     wide, long = disorder_ref.shape[1], disorder_ref.shape[2]
+    tall, vectors, extent = lattice.shape[1:]
     blocks = long // BLOCK
+    halves = vectors // 8
+    cos, sin = HOP_NEXT * TWIST_COS, HOP_NEXT * TWIST_SIN
 
     def at(a, b):
         return (lax.rem(gx + a + nx, nx), lax.rem(gy + b + ny, ny))
@@ -53,7 +57,8 @@
         )
 
     barrier = pltpu.get_barrier_semaphore()
-    greeted = [at(0, i) for i in range(1, ny)] + [at(a, b) for a, b in WAYS if a != 0]
+    greeted = [at(0, i) for i in range(1, ny)] + [at(i, 0) for i in range(1, nx)]
+    greeted += [at(a, b) for a, b in WAYS if a != 0 and b != 0]
     for device in greeted:
         pl.semaphore_signal(barrier, inc=1, device_id=device, device_id_type=MESH)
 
@@ -71,12 +76,11 @@
             block = jnp.where(wanted, turned[k], block)
         place[...] = block
 
-    order = list(range(1, ny))
-    for i in order:
+    for i in range(1, ny):
         fill(lax.rem(gy + i, ny), send.at[i])
     pl.semaphore_wait(barrier, len(greeted))
     moves = []
-    for i in order:
+    for i in range(1, ny):
         move = copy(send.at[i], recv.at[gy], a2a_send.at[i], a2a_recv.at[i], at(0, i))
         move.start()
         moves.append(move)
@@ -93,12 +97,36 @@
             move.start()
             sites.append(move)
     fill(gy, recv.at[gy])
+    traces[...] = jnp.zeros_like(traces)
+
+    for move in moves:
+        move.wait()
+    for k in range(blocks):
+        stored = plan_ref[gy * blocks + k]
+        block = recv[0]
+        for p in range(1, ny):
+            block = jnp.where(stored >= p * blocks, recv[p], block)
+        lattice[:, HALO : HALO + wide, :, k * BLOCK : (k + 1) * BLOCK] = block
+    halos = []
+    for w, (a, b) in enumerate(WAYS):
+        own = rows_to(a, wide)
+        rows = slice(own.start + HALO, own.stop + HALO)
+        if b == 0:
+            source = lattice.at[:, rows, :, 0:long]
+            target = lattice.at[:, rows_from(a, wide), :, 0:long]
+        else:
+            lanes = slice(long - BLOCK, long) if b == 1 else slice(0, BLOCK)
+            source = lattice.at[:, rows, :, lanes]
+            target = side.at[0 if b == -1 else 1, :, rows_from(a, wide)]
+        move = copy(source, target, halo_send.at[w], halo_recv.at[w], at(a, b))
+        move.start()
+        halos.append(move)
 
     for move in sites:
         move.wait()
     low = lax.broadcasted_iota(jnp.int32, (2, wide, BLOCK), 2) < BLOCK // 2
     for own, by_x, by_y, out in (
-        (disorder_ref, level_x, level_y, level_ref),
+        (disorder_ref, level_x, level_y, onsite),
         (vacancy_ref, vac_x, vac_y, keep_ref),
     ):
         for a in (-1, 0, 1):
@@ -107,54 +135,20 @@
             kept = rows_to(a, wide)
             out[:, rows_from(a, wide), 0:long] = middle[:, kept].astype(F32)
             out[:, rows_from(a, wide), long:] = edge[:, kept].astype(F32)
-
-    for move in moves:
-        move.wait()
-    for k in range(blocks):
-        stored = plan_ref[gy * blocks + k]
-        block = recv[0]
-        for p in range(1, ny):
-            block = jnp.where(stored >= p * blocks, recv[p], block)
-        grid[:, HALO : HALO + wide, :, k * BLOCK : (k + 1) * BLOCK] = block
-    halos = []
-    for w, (a, b) in enumerate(WAYS):
-        own = rows_to(a, wide)
-        rows = slice(own.start + HALO, own.stop + HALO)
-        if b == 0:
-            source, target = grid.at[:, rows, :, 0:long], grid.at[:, rows_from(a, wide), :, 0:long]
-        else:
-            lanes = slice(long - BLOCK, long) if b == 1 else slice(0, BLOCK)
-            source = grid.at[:, rows, :, lanes]
-            target = side.at[0 if b == -1 else 1, :, rows_from(a, wide)]
-        move = copy(source, target, halo_send.at[w], halo_recv.at[w], at(a, b))
-        move.start()
-        halos.append(move)
+    factor[...] = keep_ref[...] * (1.0 / SPREAD)
+    onsite[...] = onsite[...] * factor[...]
+
     for move in halos:
         move.wait()
-    low = lax.broadcasted_iota(jnp.int32, grid.shape[:3] + (BLOCK,), 3) < BLOCK // 2
-    lattice_ref[:, :, :, 0:long] = grid[...]
-    lattice_ref[:, :, :, long:] = jnp.where(
-        low, side[0].astype(F32), side[1].astype(F32)).astype(jnp.bfloat16)
-
-
-def chebyshev(
-    lattice_ref, level_ref, keep_ref, moments_ref, trace_ref,
-    real0, imag0, real1, imag1, onsite, factor, traces,
-):
-    tall, vectors, extent = lattice_ref.shape[1:]
-    wide, long = moments_ref.shape[2], moments_ref.shape[3]
-    halves = vectors // 8
-    cos, sin = HOP_NEXT * TWIST_COS, HOP_NEXT * TWIST_SIN
-
-    factor[...] = keep_ref[...] * (1.0 / SPREAD)
-    onsite[...] = level_ref[...] * factor[...]
-    traces[...] = jnp.zeros_like(traces)
+    low = lax.broadcasted_iota(jnp.int32, (vectors, BLOCK), 1) < BLOCK // 2
 
     @pl.loop(0, tall)
     def _(x):
         for s in range(2):
             mask = keep_ref[s, pl.ds(x, 1), :]
-            real0[s, x] = lattice_ref[s, x].astype(F32) * mask
+            real0[s, x, :, 0:long] = lattice[s, x, :, 0:long].astype(F32) * mask[:, 0:long]
+            edge = jnp.where(low, side[0, s, x].astype(F32), side[1, s, x].astype(F32))
+            real0[s, x, :, long:] = edge * mask[:, long:]
 
     def back(value):
         return pltpu.roll(value, 1, axis=1)
@@ -214,9 +208,9 @@
                     if keep_new:
                         store[s, x, r8, :] = result
                     if part == 0 and measured is not None:
-                        start = lattice_ref[s, x].astype(F32)[half * 8 : half * 8 + 8]
-                        start = start * keep_ref[s, pl.ds(x, 1), :]
-                        measured(s, half, start[:, :long] * result[:, :long])
+                        start = lattice[s, x, :, 0:long].astype(F32)[half * 8 : half * 8 + 8]
+                        start = start * keep_ref[s, pl.ds(x, 1), 0:long]
+                        measured(s, half, start * result[:, :long])
 
         def plain(x, carry):
             for half in range(halves):
@@ -246,11 +240,32 @@
         if n < TERMS:
             lax.fori_loop(HALO + wide, tall - n, plain, 0)
 
+    slot = lax.broadcasted_iota(jnp.int32, (vectors, BLOCK), 0)
     lane = lax.broadcasted_iota(jnp.int32, (vectors, BLOCK), 1)
-    gathered = jnp.zeros((vectors, BLOCK), F32)
+    part[...] = jnp.zeros_like(part)
     for n in range(TERMS):
-        gathered = jnp.where(lane == n, jnp.sum(traces[n], axis=1, keepdims=True), gathered)
-    trace_ref[...] = gathered
+        spread = jnp.where(slot == lane, jnp.sum(traces[n], axis=1, keepdims=True), 0.0)
+        part[0, n : n + 1, :] = jnp.sum(spread, axis=0, keepdims=True)
+
+    def gather(stage, count, me, slots, place):
+        slots[me] = part[stage]
+        sent = []
+        for i in range(1, count):
+            move = copy(part.at[stage], slots.at[me], sum_send.at[stage, i],
+                        sum_recv.at[stage, i], place(i))
+            move.start()
+            sent.append(move)
+        for move in sent:
+            move.wait()
+        total = slots[0]
+        for p in range(1, count):
+            total = total + slots[p]
+        return total
+
+    part[1] = gather(0, ny, gy, parts_y, lambda i: at(0, i))
+    total = gather(1, nx, gx, parts_x, lambda i: at(i, 0))
+    sites_total = 2 * wide * nx * long * ny
+    trace_ref[...] = total[:TERMS, :vectors] * (1.0 / sites_total)
 
 
 def local(nx, ny, stored_vectors, disorder, vacancy, plan):
@@ -259,46 +274,39 @@
     vmem = pl.BlockSpec(memory_space=pltpu.VMEM)
     bf16, i32 = jnp.bfloat16, jnp.int32
     dma = pltpu.SemaphoreType.DMA
-    ways = len(WAYS)
-    lattice, level, keep = pl.pallas_call(
-        functools.partial(exchange, nx, ny),
+    ways, most = len(WAYS), max(nx, ny)
+    return pl.pallas_call(
+        functools.partial(program, nx, ny),
         out_shape=(
-            jax.ShapeDtypeStruct((2, tall, vectors, extent), bf16),
-            jax.ShapeDtypeStruct((2, tall, extent), F32),
-            jax.ShapeDtypeStruct((2, tall, extent), F32),
+            jax.ShapeDtypeStruct((TERMS, 2, wide, long), F32),
+            jax.ShapeDtypeStruct((TERMS, vectors), F32),
         ),
         in_specs=[pl.BlockSpec(memory_space=pltpu.SMEM), vmem, vmem, vmem],
-        out_specs=(vmem,) * 3,
+        out_specs=(vmem,) * 2,
         scratch_shapes=[
             pltpu.VMEM((long // BLOCK, 2, wide, vectors, BLOCK), bf16),
             pltpu.VMEM((ny, 2, wide, vectors, BLOCK), bf16),
             pltpu.VMEM((ny, 2, wide, vectors, BLOCK), bf16),
-            pltpu.VMEM((2, tall, vectors, long), bf16),
+            pltpu.VMEM((2, tall, vectors, extent), bf16),
             pltpu.VMEM((2, 2, tall, vectors, BLOCK), bf16),
             pltpu.VMEM((ways, 2, wide, long), F32),
             pltpu.VMEM((ways, 2, wide, BLOCK), F32),
             pltpu.VMEM((ways, 2, wide, long), i32),
             pltpu.VMEM((ways, 2, wide, BLOCK), i32),
+        ]
+        + [pltpu.VMEM((2, tall, extent), F32)] * 3
+        + [pltpu.VMEM((2, tall, vectors, extent), F32)] * 4
+        + [
+            pltpu.VMEM((TERMS, vectors, BLOCK), F32),
+            pltpu.VMEM((2, 8, BLOCK), F32),
+            pltpu.VMEM((ny, 8, BLOCK), F32),
+            pltpu.VMEM((nx, 8, BLOCK), F32),
             dma((ny,)), dma((ny,)), dma((ways,)), dma((ways,)), dma((ways, 2)), dma((ways, 2)),
+            dma((2, most)), dma((2, most)),
         ],
         compiler_params=pltpu.CompilerParams(collective_id=0, has_side_effects=True),
-        name="exchange",
+        name="chebyshev",
     )(plan, stored_vectors, disorder, vacancy)
-    moments, trace = pl.pallas_call(
-        chebyshev,
-        out_shape=(
-            jax.ShapeDtypeStruct((TERMS, 2, wide, long), F32),
-            jax.ShapeDtypeStruct((vectors, BLOCK), F32),
-        ),
-        in_specs=[vmem] * 3,
-        out_specs=(vmem,) * 2,
-        scratch_shapes=[pltpu.VMEM((2, tall, vectors, extent), F32)] * 4
-        + [pltpu.VMEM((2, tall, extent), F32)] * 2
-        + [pltpu.VMEM((TERMS, vectors, BLOCK), F32)],
-        name="chebyshev",
-    )(lattice, level, keep)
-    summed = lax.psum(trace[:, :TERMS].T, ("gx", "gy"))
-    return moments, summed / (2 * wide * nx * long * ny)
 
 
 def solution(mesh):

time: 78.3 us -> 44.3 us (0.57)
  blocking collectives: 37.6 us -> 0 us
  Pallas kernels: 38.4 us -> 41.4 us
  local copies, waits for them, and re-layouts: 1.35 us -> 2.15 us
    psum x1 -> x0, blocking collectives: 37.6 us -> none  [local(): summed = lax.psum(trace[:, :TERMS].T, ('gx', 'gy'))]
    pallas_call x2 -> x1, Pallas kernels: 38.4 us -> 41.4 us  [local(): pl.pallas_call(functools.partial(program, nx, ny), out_shape=(jax.ShapeDt...]
    unnamed x1 -> x4, local copies, waits for them, and re-layouts: 0.66 us -> 2.15 us
where the time goes in v2:
time: 44.3 us; the launch traced here: 44.2 us
  Pallas kernels  41.4 us (93%)
  local copies, waits for them, and re-layouts  2.15 us (5%)
  between operations  0.65 us (1%)
    pallas_call x1, Pallas kernels, local(): pl.pallas_call(functools.partial(program, nx, ny), out_shape=(jax.ShapeDt...  41.4 us
    unnamed x4, local copies, waits for them, and re-layouts  2.15 us

profile of v2, /device:TPU:0, one launch (start us, length us, event | category | flops | bytes accessed | tf_op | source)
XLA Modules:
  0.0 44.2 jit_solution(1677956047357072629)
XLA Ops:
  0.6 41.4 %chebyshev.1 = (f32[4,2,8,512]{3,2,1,0:T(8,128)}, f32[4,16]{1,0:T(4,128)}) custom-call(s32[32]{0:T(128)} %plan_ref.1, bf16[2,16,8,512]{3,2,1,0:T(8,128)(2,1)} %stored_ref.1, f32[2,8,512]{2,1,0:T(8,128)} %disorder_ref.1, s32[2,8,512]{2,1,0:T(8,128)} %vacancy_ref.1), custom_call_target="tpu_custom_call" | custom-call | tf_op jit(solution)/shard_map/chebyshev/pallas_call | solution.py:278
  42.0 0.0 copy-start
  42.0 1.6 %copy.8 = f32[4,2,8,512]{3,2,1,0:T(8,128)} copy(f32[4,2,8,512]{3,2,1,0:T(8,128)} %get-tuple-element.4) | data formatting | bytes 262144
  43.6 0.0 copy-done
  43.6 0.6 %copy.9 = f32[4,16]{1,0:T(4,128)} copy(f32[4,16]{1,0:T(4,128)S(1)} %copy-done) | data formatting | bytes 512
Async XLA Ops:
  42.0 1.6 %copy-start = (f32[4,16]{1,0:T(4,128)S(1)}, f32[4,16]{1,0:T(4,128)}, u32[]{:S(2)}) copy-start(f32[4,16]{1,0:T(4,128)} %get-tuple-element.5) | copy-start | bytes 772

commit v3 on v2

--- a/solution.py
+++ b/solution.py
@@ -37,12 +37,13 @@
     plan_ref, stored_ref, disorder_ref, vacancy_ref,
     moments_ref, trace_ref,
     turned, send, recv, lattice, side, level_x, level_y, vac_x, vac_y, keep_ref, onsite, factor,
-    real0, imag0, real1, imag1, traces, part, parts_y, parts_x,
+    real0, real1, real2, real3, imag1, imag2, imag3, traces, packs, part, parts_y, parts_x,
     a2a_send, a2a_recv, halo_send, halo_recv, site_send, site_recv, sum_send, sum_recv,
 ):
     gx, gy = lax.axis_index("gx"), lax.axis_index("gy")
     wide, long = disorder_ref.shape[1], disorder_ref.shape[2]
-    tall, vectors, extent = lattice.shape[1:]
+    tall, vectors = lattice.shape[1:3]
+    extent = long + BLOCK
     blocks = long // BLOCK
     halves = vectors // 8
     cos, sin = HOP_NEXT * TWIST_COS, HOP_NEXT * TWIST_SIN
@@ -107,20 +108,29 @@
         for p in range(1, ny):
             block = jnp.where(stored >= p * blocks, recv[p], block)
         lattice[:, HALO : HALO + wide, :, k * BLOCK : (k + 1) * BLOCK] = block
-    halos = []
-    for w, (a, b) in enumerate(WAYS):
-        own = rows_to(a, wide)
-        rows = slice(own.start + HALO, own.stop + HALO)
+    lane = lax.broadcasted_iota(jnp.int32, (vectors, BLOCK), 1)
+    first = jnp.zeros((vectors, BLOCK), F32)
+    last = jnp.zeros((vectors, BLOCK), F32)
+    for s in range(2):
+        for x in range(wide):
+            shift = HALO * (s * wide + x)
+            tile = lattice[s, HALO + x, :, 0:BLOCK].astype(F32)
+            first = first + pltpu.roll(jnp.where(lane < HALO, tile, 0.0), shift, axis=1)
+            tile = lattice[s, HALO + x, :, long - BLOCK : long].astype(F32)
+            last = last + pltpu.roll(jnp.where(lane >= BLOCK - HALO, tile, 0.0), shift, axis=1)
+    packs[0] = first.astype(jnp.bfloat16)
+    packs[1] = last.astype(jnp.bfloat16)
+    halos = {}
+    for a, b in ((0, 1), (0, -1), (1, 0), (-1, 0), (1, 1), (1, -1), (-1, 1), (-1, -1)):
+        w = WAYS.index((a, b))
         if b == 0:
-            source = lattice.at[:, rows, :, 0:long]
-            target = lattice.at[:, rows_from(a, wide), :, 0:long]
+            own = rows_to(a, wide)
+            source = lattice.at[:, own.start + HALO : own.stop + HALO]
+            target = lattice.at[:, rows_from(a, wide)]
         else:
-            lanes = slice(long - BLOCK, long) if b == 1 else slice(0, BLOCK)
-            source = lattice.at[:, rows, :, lanes]
-            target = side.at[0 if b == -1 else 1, :, rows_from(a, wide)]
-        move = copy(source, target, halo_send.at[w], halo_recv.at[w], at(a, b))
-        move.start()
-        halos.append(move)
+            source, target = packs.at[0 if b == -1 else 1], side.at[w]
+        halos[a, b] = copy(source, target, halo_send.at[w], halo_recv.at[w], at(a, b))
+        halos[a, b].start()
 
     for move in sites:
         move.wait()
@@ -138,17 +148,18 @@
     factor[...] = keep_ref[...] * (1.0 / SPREAD)
     onsite[...] = onsite[...] * factor[...]
 
-    for move in halos:
-        move.wait()
-    low = lax.broadcasted_iota(jnp.int32, (vectors, BLOCK), 1) < BLOCK // 2
-
-    @pl.loop(0, tall)
-    def _(x):
+    def begin(a):
+        rows, own = rows_from(a, wide), rows_to(a, wide)
         for s in range(2):
-            mask = keep_ref[s, pl.ds(x, 1), :]
-            real0[s, x, :, 0:long] = lattice[s, x, :, 0:long].astype(F32) * mask[:, 0:long]
-            edge = jnp.where(low, side[0, s, x].astype(F32), side[1, s, x].astype(F32))
-            real0[s, x, :, long:] = edge * mask[:, long:]
+            for x in range(rows.start, rows.stop):
+                mask = keep_ref[s, x : x + 1, :]
+                shift = HALO * (s * wide + own.start + x - rows.start)
+                shift = (BLOCK - shift) % BLOCK
+                real0[s, x, :, 0:long] = lattice[s, x].astype(F32) * mask[:, 0:long]
+                right = pltpu.roll(side[WAYS.index((a, -1))].astype(F32), shift, axis=1)
+                left = pltpu.roll(side[WAYS.index((a, 1))].astype(F32), shift, axis=1)
+                edge = jnp.where(lane < BLOCK // 2, right, left)
+                real0[s, x, :, long:] = edge * mask[:, long:]
 
     def back(value):
         return pltpu.roll(value, 1, axis=1)
@@ -168,9 +179,11 @@
                 out_imag = out_imag + cos * (i[first] + i[second])
         return out_real, out_imag
 
-    for n in range(1, TERMS + 1):
-        cur_r, cur_i = (real0, imag0) if n % 2 else (real1, imag1)
-        new_r, new_i = (real1, imag1) if n % 2 else (real0, imag0)
+    reals_of = (real0, real1, real2, real3)
+    imags_of = (None, imag1, imag2, imag3)
+
+    def term(n, count, where, measure):
+        cur_r, cur_i = reals_of[n - 1], imags_of[n - 1]
         complex_in, want_imag, keep_new = n > 1, n < TERMS, n < TERMS
 
         def row(x, half, measured):
@@ -190,6 +203,7 @@
                 if n > 1:
                     level, scale = 2.0 * level, 2.0 * scale
                 away = 0 if s == 0 else 2
+                results = []
                 for part in range(2 if want_imag else 1):
                     own, other = (r, other_r) if part == 0 else (i, other_i)
                     hop, prior, later = here[part], behind[part], front[part]
@@ -202,30 +216,44 @@
                     result = (hop + (back(prior) + ahead(later))) * scale
                     if own is not None:
                         result = result + level * own[1]
-                    store = new_r if part == 0 else new_i
-                    if n == 2 and part == 0 or n > 2:
-                        result = result - store[s, x, r8, :]
+                    fields = reals_of if part == 0 else imags_of
+                    if n > 1 and fields[n - 2] is not None:
+                        result = result - fields[n - 2][s, x, r8, :]
                     if keep_new:
-                        store[s, x, r8, :] = result
-                    if part == 0 and measured is not None:
-                        start = lattice[s, x, :, 0:long].astype(F32)[half * 8 : half * 8 + 8]
-                        start = start * keep_ref[s, pl.ds(x, 1), 0:long]
-                        measured(s, half, start * result[:, :long])
-
-        def plain(x, carry):
+                        fields[n][s, x, r8, :] = result
+                    results.append(result[:, :long])
+                if measured is not None:
+                    measured(s, half, real0[s, x, r8, 0:long], results,
+                             r[1][:, :long], None if i is None else i[1][:, :long])
+
+        def plain(t, carry):
+            x = where(t)
             for half in range(halves):
                 row(x, half, None)
             return carry
 
-        def middle(x, carry):
+        def middle(t, carry):
+            x = where(t)
             sums = [None, None]
 
-            def measured(s, half, product):
+            def measured(s, half, start, results, now_r, now_i):
+                product = start * results[0]
                 sums[s] = product if sums[s] is None else sums[s] + product
-                total = traces[n - 1, half * 8 : half * 8 + 8, :]
-                for k in range(long // BLOCK):
-                    total = total + product[:, k * BLOCK : (k + 1) * BLOCK]
-                traces[n - 1, half * 8 : half * 8 + 8, :] = total
+                if n == 1:
+                    extra = ((0, product), (4, start * start))
+                elif n == 2:
+                    extra = (
+                        (1, product),
+                        (2, now_r * results[0] + now_i * results[1]),
+                        (3, results[0] * results[0] + results[1] * results[1]),
+                    )
+                else:
+                    extra = ()
+                for place, value in extra:
+                    total = traces[place, half * 8 : half * 8 + 8, :]
+                    for k in range(long // BLOCK):
+                        total = total + value[:, k * BLOCK : (k + 1) * BLOCK]
+                    traces[place, half * 8 : half * 8 + 8, :] = total
 
             for half in range(halves):
                 row(x, half, measured)
@@ -234,20 +262,41 @@
                     jnp.sum(sums[s], axis=0, keepdims=True) * (1.0 / vectors))
             return carry
 
-        if n < TERMS:
-            lax.fori_loop(n, HALO, plain, 0)
-        lax.fori_loop(HALO, HALO + wide, middle, 0)
-        if n < TERMS:
-            lax.fori_loop(HALO + wide, tall - n, plain, 0)
+        lax.fori_loop(0, count, middle if measure else plain, 0)
+
+    def inside(n):
+        term(n, wide - 2 * n, lambda t: HALO + n + t, True)
+
+    def border(n):
+        out = HALO - n
+        term(n, 2 * out, lambda t: n + t + wide * (t // out), False)
+        term(n, 2 * n, lambda t: HALO + t + (wide - 2 * n) * (t // n), True)
+
+    for way in ((0, 1), (0, -1)):
+        halos[way].wait()
+    begin(0)
+    for n in range(1, TERMS):
+        inside(n)
+    for way in WAYS:
+        if way[0] != 0:
+            halos[way].wait()
+    begin(-1)
+    begin(1)
+    border(1)
+    border(2)
 
     slot = lax.broadcasted_iota(jnp.int32, (vectors, BLOCK), 0)
-    lane = lax.broadcasted_iota(jnp.int32, (vectors, BLOCK), 1)
     part[...] = jnp.zeros_like(part)
     for n in range(TERMS):
-        spread = jnp.where(slot == lane, jnp.sum(traces[n], axis=1, keepdims=True), 0.0)
+        value = traces[n]
+        if n == 2:
+            value = 2.0 * value - traces[0]
+        if n == 3:
+            value = 2.0 * value - traces[4]
+        spread = jnp.where(slot == lane, jnp.sum(value, axis=1, keepdims=True), 0.0)
         part[0, n : n + 1, :] = jnp.sum(spread, axis=0, keepdims=True)
 
-    def gather(stage, count, me, slots, place):
+    def scatter(stage, count, me, slots, place):
         slots[me] = part[stage]
         sent = []
         for i in range(1, count):
@@ -255,6 +304,9 @@
                         sum_recv.at[stage, i], place(i))
             move.start()
             sent.append(move)
+        return sent
+
+    def collect(sent, count, slots):
         for move in sent:
             move.wait()
         total = slots[0]
@@ -262,8 +314,12 @@
             total = total + slots[p]
         return total
 
-    part[1] = gather(0, ny, gy, parts_y, lambda i: at(0, i))
-    total = gather(1, nx, gx, parts_x, lambda i: at(i, 0))
+    sent = scatter(0, ny, gy, parts_y, lambda i: at(0, i))
+    border(3)
+    part[1] = collect(sent, ny, parts_y)
+    sent = scatter(1, nx, gx, parts_x, lambda i: at(i, 0))
+    term(TERMS, wide, lambda t: HALO + t, True)
+    total = collect(sent, nx, parts_x)
     sites_total = 2 * wide * nx * long * ny
     trace_ref[...] = total[:TERMS, :vectors] * (1.0 / sites_total)
 
@@ -287,17 +343,18 @@
             pltpu.VMEM((long // BLOCK, 2, wide, vectors, BLOCK), bf16),
             pltpu.VMEM((ny, 2, wide, vectors, BLOCK), bf16),
             pltpu.VMEM((ny, 2, wide, vectors, BLOCK), bf16),
-            pltpu.VMEM((2, tall, vectors, extent), bf16),
-            pltpu.VMEM((2, 2, tall, vectors, BLOCK), bf16),
+            pltpu.VMEM((2, tall, vectors, long), bf16),
+            pltpu.VMEM((ways, vectors, BLOCK), bf16),
             pltpu.VMEM((ways, 2, wide, long), F32),
             pltpu.VMEM((ways, 2, wide, BLOCK), F32),
             pltpu.VMEM((ways, 2, wide, long), i32),
             pltpu.VMEM((ways, 2, wide, BLOCK), i32),
         ]
         + [pltpu.VMEM((2, tall, extent), F32)] * 3
-        + [pltpu.VMEM((2, tall, vectors, extent), F32)] * 4
+        + [pltpu.VMEM((2, tall, vectors, extent), F32)] * 7
         + [
-            pltpu.VMEM((TERMS, vectors, BLOCK), F32),
+            pltpu.VMEM((TERMS + 1, vectors, BLOCK), F32),
+            pltpu.VMEM((2, vectors, BLOCK), bf16),
             pltpu.VMEM((2, 8, BLOCK), F32),
             pltpu.VMEM((ny, 8, BLOCK), F32),
             pltpu.VMEM((nx, 8, BLOCK), F32),

time: 44.3 us -> 38.9 us (0.88)
  Pallas kernels: 41.4 us -> 36 us
    pallas_call x1, Pallas kernels: 41.4 us -> 36 us  [local(): pl.pallas_call(functools.partial(program, nx, ny), out_shape=(jax.ShapeDt...]
where the time goes in v3:
time: 38.9 us; the launch traced here: 38.8 us
  Pallas kernels  36 us (93%)
  local copies, waits for them, and re-layouts  2.15 us (6%)
  between operations  0.65 us (2%)
    pallas_call x1, Pallas kernels, local(): pl.pallas_call(functools.partial(program, nx, ny), out_shape=(jax.ShapeDt...  36 us
    unnamed x4, local copies, waits for them, and re-layouts  2.15 us

profile of v3, /device:TPU:0, one launch (start us, length us, event | category | flops | bytes accessed | tf_op | source)
XLA Modules:
  0.0 38.8 jit_solution(4419737913986395236)
XLA Ops:
  0.6 36.0 %chebyshev.1 = (f32[4,2,8,512]{3,2,1,0:T(8,128)}, f32[4,16]{1,0:T(4,128)}) custom-call(s32[32]{0:T(128)} %plan_ref.1, bf16[2,16,8,512]{3,2,1,0:T(8,128)(2,1)} %stored_ref.1, f32[2,8,512]{2,1,0:T(8,128)} %disorder_ref.1, s32[2,8,512]{2,1,0:T(8,128)} %vacancy_ref.1), custom_call_target="tpu_custom_call" | custom-call | tf_op jit(solution)/shard_map/chebyshev/pallas_call | solution.py:334
  36.6 0.0 copy-start
  36.6 1.6 %copy.8 = f32[4,2,8,512]{3,2,1,0:T(8,128)} copy(f32[4,2,8,512]{3,2,1,0:T(8,128)} %get-tuple-element.4) | data formatting | bytes 262144
  38.2 0.0 copy-done
  38.2 0.6 %copy.9 = f32[4,16]{1,0:T(4,128)} copy(f32[4,16]{1,0:T(4,128)S(1)} %copy-done) | data formatting | bytes 512
Async XLA Ops:
  36.6 1.6 %copy-start = (f32[4,16]{1,0:T(4,128)S(1)}, f32[4,16]{1,0:T(4,128)}, u32[]{:S(2)}) copy-start(f32[4,16]{1,0:T(4,128)} %get-tuple-element.5) | copy-start | bytes 772
